TPU v7x, 32 devices: a whole 2x2x4 slice. The times are simulated.
32 devices in a mesh: leaf: 32 (over z, y, x, core).
Axes of the slice: x: 2, y: 2, z: 4, core: 2. Of those that a mesh axis runs over, the one named last changes fastest.
Arguments:
- slip: bfloat16 [128, 8192], P(None, 'leaf'), may hold values from -6 to 6
- to_multipole: bfloat16 [121, 128], replicated, may hold values from -0.5 to 0.5
- up_shift: float32 [2, 121, 121], replicated, may hold values from -0.375 to 0.375
- down_shift: float32 [2, 121, 121], replicated, may hold values from -0.5 to 0.5
- sibling_far: float32 [2, 121, 121], replicated, may hold values from -0.5 to 0.5
- leaf_far: bfloat16 [27, 121, 121], replicated, may hold values from -0.25 to 0.25
- to_stress: bfloat16 [128, 121], replicated, may hold values from -0.125 to 0.125
- near_blocks: bfloat16 [9, 128, 128], replicated, may hold values from -0.1875 to 0.1875
- send_cells: int32 [32, 4096], P('leaf'), may hold values from 0 to 255, as said below
- far_list: int32 [27, 8192], P(None, 'leaf'), may hold values from 0 to 4351, as said below
- near_list: int32 [9, 8192], P(None, 'leaf'), may hold values from 0 to 319, as said below
Outputs:
- stress: float32 [128, 8192], P(None, 'leaf')
Inputs may be any that keep to these rules, and one draw needn't show every extreme that they name: `send_cells`: row q holds, in positions d * 128 to (d + 1) * 128 - 1, 128 distinct cells of device q (numbered within that device) listed for receiving device d. `far_list`: an entry v below 256 names a cell of the target's own device. Otherwise v - 256 = q * 128 + s names slot s of device q's list for the target's device, q is not the target's device, s < 128 when q lies within 4 devices of it and s < 32 when it lies farther; in every draw some entry names slot 127 of a device within 4, and some names slot 31 of a farther device. `near_list`: an entry w names the cell w - 32 counted from the first cell of the target's device, so that positions before 0 and from 256 on lie on the neighbouring devices (zeros outside the fault); entry 4 is the target itself.
All inputs are finite; a program needn't handle non-finite values.
Results may differ from a plain program's by a relative error of at most 0.0031.
Values may be sent and summed in bfloat16 or wider, within the bound.
A program may use at most 64 MiB of HBM per device.

v0:
```python
import functools

import jax
import jax.numpy as jnp
from jax import lax
from jax.experimental import pallas as pl
from jax.experimental.pallas import tpu as pltpu
from jax.sharding import PartitionSpec as P

HALO = 32
PEERS = 4
CAP_FAR = 32
LANES = 128
BF = jnp.bfloat16
F32 = jnp.float32
MESH = pl.DeviceIdType.MESH
OFFSETS = tuple(range(-PEERS, 0)) + tuple(range(1, PEERS + 1))


def mm(a, b):
    return jnp.dot(a, b, preferred_element_type=F32)


def halves(x):
    high = x.astype(BF)
    return high, (x - high.astype(F32)).astype(BF)


def one_hot(rows, index):
    count = index.shape[1]
    lines = lax.broadcasted_iota(jnp.int32, (rows, count), 0).astype(F32).astype(BF)
    hit = lines == jnp.broadcast_to(index.astype(BF), (rows, count))
    return jnp.where(hit, jnp.ones((), BF), jnp.zeros((), BF))


def kernel(
    n, cells, cap,
    slip_ref, tm_ref, up_ref, down_ref, sib_ref, leaf_any, ts_ref, nb_any, send_ref, far_ref, near_ref,
    out_ref,
    outgoing, far_buf, near_buf, edges, halo, root_out, roots,
    weight, w_up, w_sib, w_down, agg, terms, loc, rel, near_rel, source, leaf_cat, columns, near_cols, leaf_ref, nb_ref, load_sem,
    far_send, far_recv, near_send, near_recv, halo_send, halo_recv, root_send, root_recv,
):
    me = lax.axis_index("leaf")
    coef = tm_ref.shape[0]
    types = far_ref.shape[0]
    kinds = near_ref.shape[0]
    rest = cap - CAP_FAR

    loads = (
        pltpu.make_async_copy(leaf_any, leaf_ref, load_sem.at[0]),
        pltpu.make_async_copy(nb_any, nb_ref, load_sem.at[1]),
    )
    for copy in loads:
        copy.start()

    barrier = pltpu.get_barrier_semaphore()

    far_buf[...] = jnp.zeros_like(far_buf)
    near_buf[...] = jnp.zeros_like(near_buf)
    halo[...] = jnp.zeros_like(halo)

    def greet(k, carry):
        pl.semaphore_signal(barrier, inc=1, device_id=(lax.rem(me + k, n),), device_id_type=MESH)
        return carry

    lax.fori_loop(1, n, greet, 0)

    edges[0] = slip_ref[:, :LANES].astype(F32).T[:HALO].astype(BF)
    edges[1] = slip_ref[:, cells - LANES :].astype(F32).T[LANES - HALO :].astype(BF)

    weight[...] = jnp.zeros_like(weight)
    weight[0, :coef, :] = tm_ref[...].astype(F32)
    multipole = mm(weight[0].astype(BF), slip_ref[...]).astype(BF)
    source[:, :cells] = multipole

    def far_copy(k):
        target = lax.rem(me + k, n)
        return pltpu.make_async_remote_copy(
            src_ref=outgoing.at[pl.ds(pl.multiple_of(target * cap, cap), CAP_FAR)],
            dst_ref=far_buf.at[pl.ds(pl.multiple_of(me * CAP_FAR, CAP_FAR), CAP_FAR)],
            send_sem=far_send.at[k],
            recv_sem=far_recv.at[k],
            device_id=(target,),
            device_id_type=MESH,
        )

    def near_copy(j):
        target = jnp.clip(me + OFFSETS[j], 0, n - 1)
        back = len(OFFSETS) - 1 - j
        return pltpu.make_async_remote_copy(
            src_ref=outgoing.at[pl.ds(pl.multiple_of(target * cap + CAP_FAR, CAP_FAR), rest)],
            dst_ref=near_buf.at[pl.ds(back * rest, rest)],
            send_sem=near_send.at[j],
            recv_sem=near_recv.at[back],
            device_id=(target,),
            device_id_type=MESH,
        )

    def halo_copy(side):
        target = jnp.clip(me + (1 if side else -1), 0, n - 1)
        return pltpu.make_async_remote_copy(
            src_ref=edges.at[side],
            dst_ref=halo.at[pl.ds((1 - side) * HALO, HALO)],
            send_sem=halo_send.at[side],
            recv_sem=halo_recv.at[1 - side],
            device_id=(target,),
            device_id_type=MESH,
        )

    def root_copy(k):
        return pltpu.make_async_remote_copy(
            src_ref=root_out,
            dst_ref=roots.at[me],
            send_sem=root_send.at[k],
            recv_sem=root_recv.at[k],
            device_id=(lax.rem(me + k, n),),
            device_id_type=MESH,
        )

    def inside(offset):
        return jnp.logical_and(me + offset >= 0, me + offset < n)

    def parts(ref, index):
        weight[index, :coef, :coef] = ref
        weight[index, :coef, coef:] = jnp.zeros((coef, LANES - coef), F32)
        return halves(weight[index].T)

    w_sib[...] = jnp.zeros_like(w_sib)
    for s in (0, 1):
        high, low = parts(up_ref[:, s, :], 0 + s)
        w_up[s * LANES : (s + 1) * LANES, :LANES] = high
        w_up[s * LANES : (s + 1) * LANES, LANES:] = low
        high, low = parts(down_ref[:, s, :], 2 + s)
        w_down[:LANES, s * LANES : (s + 1) * LANES] = high
        w_down[LANES:, s * LANES : (s + 1) * LANES] = low
        high, low = parts(sib_ref[:, s, :], 4 + s)
        other = 1 - s
        w_sib[0, other * LANES : (other + 1) * LANES, s * LANES : (s + 1) * LANES] = high
        w_sib[1, other * LANES : (other + 1) * LANES, s * LANES : (s + 1) * LANES] = low

    def pair(base, rows):
        m = max(rows // 2, 8)
        even = agg[pl.ds(base, m, stride=2), :]
        odd = agg[pl.ds(base + 1, m, stride=2), :]
        return m, halves(jnp.concatenate([even, odd], axis=1))

    def lift(high, low):
        first = mm(high, w_up[...])
        second = mm(low, w_up[:, :LANES])
        return first[:, :LANES] + first[:, LANES:] + second

    def across(high, low):
        return mm(high, w_sib[0]) + mm(high, w_sib[1]) + mm(low, w_sib[0])

    def place(base, value):
        agg[base : base + value.shape[0], :] = value
        if value.shape[0] < 16:
            agg[base + value.shape[0] : base + 16, :] = jnp.zeros((16 - value.shape[0], LANES), F32)

    local_levels = cells.bit_length() - 1
    tree_bits = n.bit_length() - 1
    base, spot = 0, 0
    agg[:cells, :] = multipole.astype(F32).T
    local_spots = []
    for height in range(local_levels):
        rows = cells >> height
        m, (high, low) = pair(base, rows)
        if height >= 1:
            terms[spot : spot + m, :] = across(high, low)
            local_spots.append(spot)
            spot += m
        else:
            local_spots.append(None)
        value = lift(high, low)
        base += max(rows, 16)
        place(base, value)
    root_out[...] = value[:1]
    roots[me] = value[:1]

    chunk = 4 * cap
    for start in range(0, n * cap, chunk):
        picked = one_hot(cells, send_ref[0:1, start : start + chunk].astype(F32))
        outgoing[start : start + chunk, :] = mm(multipole, picked).T.astype(BF)

    v = far_ref[...]
    behind = v - cells
    sender = behind // cap
    slot = behind % cap
    delta = sender - me
    lane = jnp.where(delta < 0, delta + PEERS, delta + PEERS - 1)
    position = jnp.where(
        v < cells,
        v,
        jnp.where(
            slot < CAP_FAR,
            cells + near_buf.shape[0] + sender * CAP_FAR + slot,
            cells + lane * rest + slot - CAP_FAR,
        ),
    )
    total = source.shape[1]
    blocks = total // 256
    for b in range(blocks):
        rel[b, :types, :] = jnp.clip(position - 256 * b, -1, 256).astype(F32)

    w = near_ref[...]
    near_rel[0, :kinds, :] = jnp.clip(w - HALO, -1, cells).astype(F32)
    near_rel[1, :kinds, :] = jnp.where(
        w < HALO, w, jnp.where(w >= HALO + cells, w - cells, -1)
    ).astype(F32)
    slips = slip_ref[...]
    for k in range(kinds):
        near_cols[k * LANES : (k + 1) * LANES, :] = mm(
            slips, one_hot(cells, near_rel[0, k : k + 1, :])
        ).astype(BF)

    group = 3 if types % 3 == 0 else 1

    def gather(low, high, more):
        def step(g, carry):
            for i in range(group):
                t = g * group + i
                hits = jnp.concatenate(
                    [one_hot(256, rel[b, pl.ds(t, 1), :]) for b in range(low, high)], axis=0
                )
                picked = mm(source[:, low * 256 : high * 256], hits).astype(BF)
                rows = pl.ds(pl.multiple_of(t * LANES, LANES), LANES)
                if more:
                    picked = picked + columns[rows, :]
                columns[rows, :] = picked
            return carry

        lax.fori_loop(0, types // group, step, 0)

    gather(0, cells // 256, False)

    for copy in loads:
        copy.wait()
    leaf_cat[...] = jnp.zeros_like(leaf_cat)
    for t in range(types):
        leaf_cat[:coef, t * LANES : t * LANES + coef] = leaf_ref[t]

    pl.semaphore_wait(barrier, n - 1)

    def start_root(k, carry):
        root_copy(k).start()
        return carry

    lax.fori_loop(1, n, start_root, 0)
    for side in (0, 1):
        @pl.when(inside(1 if side else -1))
        def _():
            halo_copy(side).start()

    for j, offset in enumerate(OFFSETS):
        @pl.when(inside(offset))
        def _():
            near_copy(j).start()
    def start_far(k, carry):
        far_copy(lax.rem(k + n // 2 - 2, n - 1) + 1).start()
        return carry

    lax.fori_loop(1, n, start_far, 0)

    for j, offset in enumerate(OFFSETS):
        @pl.when(inside(offset))
        def _():
            near_copy(j).wait_send()

        @pl.when(inside(OFFSETS[len(OFFSETS) - 1 - j]))
        def _():
            near_copy(j).wait_recv()

    close = cells + near_buf.shape[0]
    source[:, cells:close] = near_buf[...].astype(F32).T.astype(BF)
    gather(cells // 256, close // 256, True)

    for side in (0, 1):
        @pl.when(inside(1 if side else -1))
        def _():
            halo_copy(side).wait_send()

        @pl.when(inside(-1 if side else 1))
        def _():
            halo_copy(side).wait_recv()

    side_slips = jnp.concatenate(
        [halo[...], jnp.zeros((LANES - 2 * HALO, LANES), BF)], axis=0
    ).astype(F32).T.astype(BF)
    stress = jnp.zeros(out_ref.shape, F32)
    for k in range(kinds):
        column = near_cols[k * LANES : (k + 1) * LANES, :] + mm(
            side_slips, one_hot(LANES, near_rel[1, k : k + 1, :])
        ).astype(BF)
        stress = stress + mm(nb_ref[k], column)
    out_ref[...] = stress

    def wait_root(k, carry):
        root_copy(k).wait()
        return carry

    lax.fori_loop(1, n, wait_root, 0)
    base = 0
    place(base, roots[:, 0, :])
    tree_spots = []
    for bit in range(tree_bits):
        rows = n >> bit
        m, (high, low) = pair(base, rows)
        terms[spot : spot + m, :] = across(high, low)
        tree_spots.append(spot)
        spot += m
        if bit + 1 < tree_bits:
            value = lift(high, low)
            base += max(rows, 16)
            place(base, value)

    def descend(x):
        high, low = halves(x)
        return mm(high, w_down[:LANES, :]) + mm(high, w_down[LANES:, :]) + mm(low, w_down[:LANES, :])

    expansion = jnp.zeros((8, LANES), F32)
    for bit in reversed(range(tree_bits)):
        both = terms[pl.ds(tree_spots[bit] + (me >> (bit + 1)), 1), :]
        both = jnp.broadcast_to(both, (8, 2 * LANES))
        if bit + 1 < tree_bits:
            both = both + descend(expansion)
        expansion = jnp.where((me >> bit) & 1 == 0, both[:, :LANES], both[:, LANES:])
    for height in reversed(range(local_levels)):
        m = max((cells >> height) // 2, 8)
        both = descend(expansion)
        if height >= 1:
            both = both + terms[local_spots[height] : local_spots[height] + m, :]
        loc[pl.ds(0, m, stride=2), :] = both[:, :LANES]
        loc[pl.ds(1, m, stride=2), :] = both[:, LANES:]
        expansion = loc[: max(cells >> height, 8), :]

    def wait_far(k, carry):
        far_copy(k).wait()
        return carry

    lax.fori_loop(1, n, wait_far, 0)
    source[:, close:] = far_buf[...].astype(F32).T.astype(BF)
    gather(close // 256, blocks, True)
    leaf_sum = mm(leaf_cat[...], columns[...])
    local_exp = (expansion.T + leaf_sum)[:coef].astype(BF)
    out_ref[...] = out_ref[...] + mm(ts_ref[...], local_exp)


def round_up(value, unit):
    return -(-value // unit) * unit


def body(*args):
    slip, _, _, _, _, leaf_far, _, near_blocks, send_cells, far_list, near_list = args
    n = lax.axis_size("leaf")
    cells = slip.shape[1]
    cap = send_cells.shape[1] // n
    rest = cap - CAP_FAR
    peers = len(OFFSETS)
    total = cells + n * CAP_FAR + peers * rest
    dma = pltpu.SemaphoreType.DMA
    return pl.pallas_call(
        functools.partial(kernel, n, cells, cap),
        out_shape=jax.ShapeDtypeStruct(slip.shape, F32),
        in_specs=[
            pl.BlockSpec(memory_space=pl.ANY if i in (5, 7) else pltpu.VMEM) for i in range(len(args))
        ],
        out_specs=pl.BlockSpec(memory_space=pltpu.VMEM),
        scratch_shapes=[
            pltpu.VMEM((n * cap, LANES), BF),
            pltpu.VMEM((n * CAP_FAR, LANES), BF),
            pltpu.VMEM((peers * rest, LANES), BF),
            pltpu.VMEM((2, HALO, LANES), BF),
            pltpu.VMEM((2 * HALO, LANES), BF),
            pltpu.VMEM((1, LANES), F32),
            pltpu.VMEM((n, 1, LANES), F32),
            pltpu.VMEM((6, LANES, LANES), F32),
            pltpu.VMEM((2 * LANES, 2 * LANES), BF),
            pltpu.VMEM((2, 2 * LANES, 2 * LANES), BF),
            pltpu.VMEM((2 * LANES, 2 * LANES), BF),
            pltpu.VMEM((2 * cells + 2 * n + 128, LANES), F32),
            pltpu.VMEM((cells + n + 128, 2 * LANES), F32),
            pltpu.VMEM((cells, LANES), F32),
            pltpu.VMEM((total // 256, round_up(far_list.shape[0], 8), cells), F32),
            pltpu.VMEM((2, round_up(near_list.shape[0], 8), cells), F32),
            pltpu.VMEM((LANES, total), BF),
            pltpu.VMEM((LANES, far_list.shape[0] * LANES), BF),
            pltpu.VMEM((far_list.shape[0] * LANES, cells), BF),
            pltpu.VMEM((near_list.shape[0] * LANES, cells), BF),
            pltpu.VMEM(leaf_far.shape, BF),
            pltpu.VMEM(near_blocks.shape, BF),
            dma((2,)),
            dma((n,)),
            dma((n,)),
            dma((peers,)),
            dma((peers,)),
            dma((2,)),
            dma((2,)),
            dma((n,)),
            dma((n,)),
        ],
        compiler_params=pltpu.CompilerParams(collective_id=0, has_side_effects=True),
    )(*(jnp.transpose(a, (1, 0, 2)) if 2 <= i < 5 else a for i, a in enumerate(args)))


def solution(mesh):
    return jax.shard_map(
        body,
        mesh=mesh,
        in_specs=(
            P(None, "leaf"),
            P(),
            P(),
            P(),
            P(),
            P(),
            P(),
            P(),
            P("leaf", None),
            P(None, "leaf"),
            P(None, "leaf"),
        ),
        out_specs=P(None, "leaf"),
        check_vma=False,
    )
```

profile of v0, /device:TPU:11, one launch (start us, length us, event | category | flops | bytes accessed | tf_op | source)
XLA Modules:
  0.0 28.2 jit_solution(3937349822182096116)
XLA Ops:
  0.0 26.7 %shard_map.109 = f32[128,256]{1,0:T(8,128)} custom-call(bf16[128,256]{1,0:T(8,128)(2,1)} %slip_ref.1, bf16[121,128]{1,0:T(8,128)(2,1)} %tm_ref.1, f32[121,2,121]{2,1,0:T(2,128)} %bitcast.3, f32[121,2,121]{2,1,0:T(2,128)} %bitcast.4, f32[121,2,121]{2,1,0:T(2,128)} %bitcast.5, bf16[27,121,121]{2,1,0:T(8,128)(2,1)} %leaf_any.1, bf16[128,121]{1,0:T(8,128)(2,1)} %ts_ref.1, ...), custom_call_target="tpu_custom_call" | custom-call | tf_op jit(solution)/shard_map/pallas_call | solution.py:362
  26.7 1.6 %copy.13 = f32[128,256]{1,0:T(8,128)} copy(f32[128,256]{1,0:T(8,128)} %shard_map.109) | data formatting | bytes 262144
where the time goes:
time: 28.4 us; the launch traced here: 28.2 us
  Pallas kernels  26.7 us (94%)
  local copies, waits for them, and re-layouts  1.57 us (6%)
    pallas_call x1, Pallas kernels, body(): pl.pallas_call(functools.partial(kernel, n, cells, cap), out_shape=jax.Sh...  26.7 us
    unnamed x1, local copies, waits for them, and re-layouts  1.57 us

commit v1 on v0

--- a/solution.py
+++ b/solution.py
@@ -35,10 +35,11 @@
 
 def kernel(
     n, cells, cap,
-    slip_ref, tm_ref, up_ref, down_ref, sib_ref, leaf_any, ts_ref, nb_any, send_ref, far_ref, near_ref,
+    slip_any, tm_any, up_any, down_any, sib_any, leaf_any, ts_any, nb_any, send_any, far_any, near_any,
     out_ref,
-    outgoing, far_buf, near_buf, edges, halo, root_out, roots,
-    weight, w_up, w_sib, w_down, agg, terms, loc, rel, near_rel, source, leaf_cat, columns, near_cols, leaf_ref, nb_ref, load_sem,
+    slip_ref, tm_ref, up_ref, down_ref, sib_ref, leaf_ref, ts_ref, nb_ref, send_ref, far_ref, near_ref,
+    far_out, near_out, far_buf, near_buf, edges, halo, root_out, roots, send_f, far_idx,
+    weight, w_up, w_sib, w_down, agg, terms, loc, rel, near_rel, source, leaf_cat, columns, near_cols, load_sem,
     far_send, far_recv, near_send, near_recv, halo_send, halo_recv, root_send, root_recv,
 ):
     me = lax.axis_index("leaf")
@@ -46,11 +47,16 @@
     types = far_ref.shape[0]
     kinds = near_ref.shape[0]
     rest = cap - CAP_FAR
-
-    loads = (
-        pltpu.make_async_copy(leaf_any, leaf_ref, load_sem.at[0]),
-        pltpu.make_async_copy(nb_any, nb_ref, load_sem.at[1]),
+    team = 256 // CAP_FAR
+    teams = n // team
+    mine = me // team
+
+    pairs = (
+        (slip_any, slip_ref), (tm_any, tm_ref), (send_any, send_ref), (up_any, up_ref), (sib_any, sib_ref),
+        (far_any, far_ref), (near_any, near_ref), (down_any, down_ref), (leaf_any, leaf_ref), (nb_any, nb_ref),
+        (ts_any, ts_ref),
     )
+    loads = [pltpu.make_async_copy(a, b, load_sem.at[i]) for i, (a, b) in enumerate(pairs)]
     for copy in loads:
         copy.start()
 
@@ -66,22 +72,34 @@
 
     lax.fori_loop(1, n, greet, 0)
 
-    edges[0] = slip_ref[:, :LANES].astype(F32).T[:HALO].astype(BF)
-    edges[1] = slip_ref[:, cells - LANES :].astype(F32).T[LANES - HALO :].astype(BF)
-
     weight[...] = jnp.zeros_like(weight)
+    w_sib[...] = jnp.zeros_like(w_sib)
+    for copy in loads[:3]:
+        copy.wait()
+
     weight[0, :coef, :] = tm_ref[...].astype(F32)
     multipole = mm(weight[0].astype(BF), slip_ref[...]).astype(BF)
     source[:, :cells] = multipole
-
-    def far_copy(k):
-        target = lax.rem(me + k, n)
+    edges[0] = slip_ref[:, :LANES].astype(F32).T[:HALO].astype(BF)
+    edges[1] = slip_ref[:, cells - LANES :].astype(F32).T[LANES - HALO :].astype(BF)
+
+    def far_copy(target):
         return pltpu.make_async_remote_copy(
-            src_ref=outgoing.at[pl.ds(pl.multiple_of(target * cap, cap), CAP_FAR)],
+            src_ref=far_out.at[pl.ds(pl.multiple_of(target * CAP_FAR, CAP_FAR), CAP_FAR)],
             dst_ref=far_buf.at[pl.ds(pl.multiple_of(me * CAP_FAR, CAP_FAR), CAP_FAR)],
-            send_sem=far_send.at[k],
-            recv_sem=far_recv.at[k],
+            send_sem=far_send,
+            recv_sem=far_recv.at[mine],
             device_id=(target,),
+            device_id_type=MESH,
+        )
+
+    def far_rows(start, rows, team_index):
+        return pltpu.make_async_remote_copy(
+            src_ref=far_out.at[pl.ds(start, rows)],
+            dst_ref=far_buf.at[pl.ds(start, rows)],
+            send_sem=far_send,
+            recv_sem=far_recv.at[team_index],
+            device_id=(lax.rem(me + 1, n),),
             device_id_type=MESH,
         )
 
@@ -89,7 +107,7 @@
         target = jnp.clip(me + OFFSETS[j], 0, n - 1)
         back = len(OFFSETS) - 1 - j
         return pltpu.make_async_remote_copy(
-            src_ref=outgoing.at[pl.ds(pl.multiple_of(target * cap + CAP_FAR, CAP_FAR), rest)],
+            src_ref=near_out.at[pl.ds(j * cap + CAP_FAR, rest)],
             dst_ref=near_buf.at[pl.ds(back * rest, rest)],
             send_sem=near_send.at[j],
             recv_sem=near_recv.at[back],
@@ -121,19 +139,65 @@
     def inside(offset):
         return jnp.logical_and(me + offset >= 0, me + offset < n)
 
+    send_f[...] = send_ref[...].astype(F32)
+    per_row = LANES // CAP_FAR
+    strip = 8 * per_row
+    lane = lax.broadcasted_iota(jnp.int32, (8, LANES), 1)
+    for g in range(n // strip):
+        packed = send_f[pl.ds(g * strip, 8, stride=per_row), :]
+        for j in range(1, per_row):
+            shifted = pltpu.roll(send_f[pl.ds(g * strip + j, 8, stride=per_row), :], j * CAP_FAR, axis=1)
+            packed = jnp.where(lane >= j * CAP_FAR, shifted, packed)
+        far_idx[g * 8 : (g + 1) * 8, :] = packed
+
+    def pick(first, second):
+        hits = jnp.concatenate([one_hot(cells, first), one_hot(cells, second)], axis=1)
+        return mm(multipole, hits).T.astype(BF)
+
+    for g in range(n // (2 * per_row)):
+        far_out[g * 256 : (g + 1) * 256, :] = pick(far_idx[2 * g : 2 * g + 1, :], far_idx[2 * g + 1 : 2 * g + 2, :])
+
+    for j in range(0, len(OFFSETS), 2):
+        first, second = (
+            send_f[pl.ds(jnp.clip(me + OFFSETS[i], 0, n - 1), 1), :] for i in (j, j + 1)
+        )
+        near_out[j * cap : (j + 2) * cap, :] = pick(first, second)
+
+    pl.semaphore_wait(barrier, n - 1)
+
+    for j, offset in enumerate(OFFSETS):
+        @pl.when(inside(offset))
+        def _():
+            near_copy(j).start()
+
+    def start_far(i, carry):
+        target = (i // team) * team + lax.rem(me + i, team)
+
+        @pl.when(target != me)
+        def _():
+            far_copy(target).start()
+
+        return carry
+
+    lax.fori_loop(0, n, start_far, 0)
+
+    for side in (0, 1):
+        @pl.when(inside(1 if side else -1))
+        def _():
+            halo_copy(side).start()
+
+    for copy in loads[3:5]:
+        copy.wait()
+
     def parts(ref, index):
         weight[index, :coef, :coef] = ref
         weight[index, :coef, coef:] = jnp.zeros((coef, LANES - coef), F32)
         return halves(weight[index].T)
 
-    w_sib[...] = jnp.zeros_like(w_sib)
     for s in (0, 1):
         high, low = parts(up_ref[:, s, :], 0 + s)
         w_up[s * LANES : (s + 1) * LANES, :LANES] = high
         w_up[s * LANES : (s + 1) * LANES, LANES:] = low
-        high, low = parts(down_ref[:, s, :], 2 + s)
-        w_down[:LANES, s * LANES : (s + 1) * LANES] = high
-        w_down[LANES:, s * LANES : (s + 1) * LANES] = low
         high, low = parts(sib_ref[:, s, :], 4 + s)
         other = 1 - s
         w_sib[0, other * LANES : (other + 1) * LANES, s * LANES : (s + 1) * LANES] = high
@@ -178,24 +242,34 @@
     root_out[...] = value[:1]
     roots[me] = value[:1]
 
-    chunk = 4 * cap
-    for start in range(0, n * cap, chunk):
-        picked = one_hot(cells, send_ref[0:1, start : start + chunk].astype(F32))
-        outgoing[start : start + chunk, :] = mm(multipole, picked).T.astype(BF)
+    def start_root(k, carry):
+        root_copy(k).start()
+        return carry
+
+    lax.fori_loop(1, n, start_root, 0)
+
+    for copy in loads[5:]:
+        copy.wait()
+
+    for s in (0, 1):
+        high, low = parts(down_ref[:, s, :], 2 + s)
+        w_down[:LANES, s * LANES : (s + 1) * LANES] = high
+        w_down[LANES:, s * LANES : (s + 1) * LANES] = low
 
     v = far_ref[...]
     behind = v - cells
     sender = behind // cap
     slot = behind % cap
     delta = sender - me
-    lane = jnp.where(delta < 0, delta + PEERS, delta + PEERS - 1)
+    close = cells + near_buf.shape[0]
+    hop = jnp.where(delta < 0, delta + PEERS, delta + PEERS - 1)
     position = jnp.where(
         v < cells,
         v,
         jnp.where(
             slot < CAP_FAR,
-            cells + near_buf.shape[0] + sender * CAP_FAR + slot,
-            cells + lane * rest + slot - CAP_FAR,
+            close + sender * CAP_FAR + slot,
+            cells + hop * rest + slot - CAP_FAR,
         ),
     )
     total = source.shape[1]
@@ -214,16 +288,16 @@
             slips, one_hot(cells, near_rel[0, k : k + 1, :])
         ).astype(BF)
 
-    group = 3 if types % 3 == 0 else 1
-
-    def gather(low, high, more):
+    group = 27
+
+    def gather(low, count, more):
         def step(g, carry):
             for i in range(group):
                 t = g * group + i
                 hits = jnp.concatenate(
-                    [one_hot(256, rel[b, pl.ds(t, 1), :]) for b in range(low, high)], axis=0
+                    [one_hot(256, rel[low + b, pl.ds(t, 1), :]) for b in range(count)], axis=0
                 )
-                picked = mm(source[:, low * 256 : high * 256], hits).astype(BF)
+                picked = mm(source[:, pl.ds(pl.multiple_of(low * 256, 256), count * 256)], hits).astype(BF)
                 rows = pl.ds(pl.multiple_of(t * LANES, LANES), LANES)
                 if more:
                     picked = picked + columns[rows, :]
@@ -234,46 +308,21 @@
 
     gather(0, cells // 256, False)
 
-    for copy in loads:
-        copy.wait()
     leaf_cat[...] = jnp.zeros_like(leaf_cat)
     for t in range(types):
         leaf_cat[:coef, t * LANES : t * LANES + coef] = leaf_ref[t]
 
-    pl.semaphore_wait(barrier, n - 1)
-
-    def start_root(k, carry):
-        root_copy(k).start()
-        return carry
-
-    lax.fori_loop(1, n, start_root, 0)
-    for side in (0, 1):
-        @pl.when(inside(1 if side else -1))
-        def _():
-            halo_copy(side).start()
-
     for j, offset in enumerate(OFFSETS):
         @pl.when(inside(offset))
         def _():
-            near_copy(j).start()
-    def start_far(k, carry):
-        far_copy(lax.rem(k + n // 2 - 2, n - 1) + 1).start()
-        return carry
-
-    lax.fori_loop(1, n, start_far, 0)
-
-    for j, offset in enumerate(OFFSETS):
-        @pl.when(inside(offset))
-        def _():
             near_copy(j).wait_send()
 
         @pl.when(inside(OFFSETS[len(OFFSETS) - 1 - j]))
         def _():
             near_copy(j).wait_recv()
 
-    close = cells + near_buf.shape[0]
     source[:, cells:close] = near_buf[...].astype(F32).T.astype(BF)
-    gather(cells // 256, close // 256, True)
+    gather(cells // 256, near_buf.shape[0] // 256, True)
 
     for side in (0, 1):
         @pl.when(inside(1 if side else -1))
@@ -334,16 +383,27 @@
         loc[pl.ds(1, m, stride=2), :] = both[:, LANES:]
         expansion = loc[: max(cells >> height, 8), :]
 
-    def wait_far(k, carry):
-        far_copy(k).wait()
+    def take_team(i, carry):
+        index = mine ^ i
+        start = pl.multiple_of(index * 256, 256)
+
+        @pl.when(i == 0)
+        def _():
+            far_rows(start, 256 - CAP_FAR, index).wait_recv()
+
+        @pl.when(i != 0)
+        def _():
+            far_rows(start, 256, index).wait_recv()
+
+        source[:, pl.ds(close + start, 256)] = far_buf[pl.ds(start, 256), :].astype(F32).T.astype(BF)
+        gather(close // 256 + index, 1, True)
         return carry
 
-    lax.fori_loop(1, n, wait_far, 0)
-    source[:, close:] = far_buf[...].astype(F32).T.astype(BF)
-    gather(close // 256, blocks, True)
+    lax.fori_loop(0, teams, take_team, 0)
     leaf_sum = mm(leaf_cat[...], columns[...])
     local_exp = (expansion.T + leaf_sum)[:coef].astype(BF)
     out_ref[...] = out_ref[...] + mm(ts_ref[...], local_exp)
+    far_rows(0, (n - 1) * CAP_FAR, 0).wait_send()
 
 
 def round_up(value, unit):
@@ -351,29 +411,34 @@
 
 
 def body(*args):
-    slip, _, _, _, _, leaf_far, _, near_blocks, send_cells, far_list, near_list = args
+    args = list(args)
     n = lax.axis_size("leaf")
-    cells = slip.shape[1]
-    cap = send_cells.shape[1] // n
+    cells = args[0].shape[1]
+    cap = args[8].shape[1] // n
+    for i in (2, 3, 4):
+        args[i] = jnp.transpose(args[i], (1, 0, 2))
+    args[8] = jnp.reshape(args[8], (n, cap))
+    slip, far_list, near_list = args[0], args[9], args[10]
     rest = cap - CAP_FAR
     peers = len(OFFSETS)
     total = cells + n * CAP_FAR + peers * rest
     dma = pltpu.SemaphoreType.DMA
     return pl.pallas_call(
         functools.partial(kernel, n, cells, cap),
-        out_shape=jax.ShapeDtypeStruct(slip.shape, F32),
-        in_specs=[
-            pl.BlockSpec(memory_space=pl.ANY if i in (5, 7) else pltpu.VMEM) for i in range(len(args))
-        ],
+        out_shape=pltpu.VMEM(slip.shape, F32),
+        in_specs=[pl.BlockSpec(memory_space=pl.ANY)] * len(args),
         out_specs=pl.BlockSpec(memory_space=pltpu.VMEM),
-        scratch_shapes=[
-            pltpu.VMEM((n * cap, LANES), BF),
+        scratch_shapes=[pltpu.VMEM(a.shape, a.dtype) for a in args] + [
+            pltpu.VMEM((n * CAP_FAR, LANES), BF),
+            pltpu.VMEM((peers * cap, LANES), BF),
             pltpu.VMEM((n * CAP_FAR, LANES), BF),
             pltpu.VMEM((peers * rest, LANES), BF),
             pltpu.VMEM((2, HALO, LANES), BF),
             pltpu.VMEM((2 * HALO, LANES), BF),
             pltpu.VMEM((1, LANES), F32),
             pltpu.VMEM((n, 1, LANES), F32),
+            pltpu.VMEM((n, cap), F32),
+            pltpu.VMEM((n * CAP_FAR // LANES, LANES), F32),
             pltpu.VMEM((6, LANES, LANES), F32),
             pltpu.VMEM((2 * LANES, 2 * LANES), BF),
             pltpu.VMEM((2, 2 * LANES, 2 * LANES), BF),
@@ -387,11 +452,9 @@
             pltpu.VMEM((LANES, far_list.shape[0] * LANES), BF),
             pltpu.VMEM((far_list.shape[0] * LANES, cells), BF),
             pltpu.VMEM((near_list.shape[0] * LANES, cells), BF),
-            pltpu.VMEM(leaf_far.shape, BF),
-            pltpu.VMEM(near_blocks.shape, BF),
-            dma((2,)),
-            dma((n,)),
-            dma((n,)),
+            dma((len(args),)),
+            dma,
+            dma((n * CAP_FAR // 256,)),
             dma((peers,)),
             dma((peers,)),
             dma((2,)),
@@ -400,7 +463,7 @@
             dma((n,)),
         ],
         compiler_params=pltpu.CompilerParams(collective_id=0, has_side_effects=True),
-    )(*(jnp.transpose(a, (1, 0, 2)) if 2 <= i < 5 else a for i, a in enumerate(args)))
+    )(*args)
 
 
 def solution(mesh):

time: 28.4 us -> 24.3 us (0.86)
  the two profiles are of different devices: /device:TPU:11 before, /device:TPU:0 now
where the time goes in v1:
time: 24.3 us; the launch traced here: 24.2 us
  Pallas kernels  23.5 us (97%)
  local copies, waits for them, and re-layouts  0.66 us (3%)
    pallas_call x1, Pallas kernels, body(): pl.pallas_call(functools.partial(kernel, n, cells, cap), out_shape=pltpu....  23.5 us
    unnamed x1, local copies, waits for them, and re-layouts  0.66 us

profile of v1, /device:TPU:0, one launch (start us, length us, event | category | flops | bytes accessed | tf_op | source)
XLA Modules:
  0.0 24.2 jit_solution(15507964000640248468)
XLA Ops:
  0.0 23.5 %shard_map.109 = f32[128,256]{1,0:T(8,128)S(1)} custom-call(bf16[128,256]{1,0:T(8,128)(2,1)} %slip_any.1, bf16[121,128]{1,0:T(8,128)(2,1)} %tm_any.1, f32[121,2,121]{2,1,0:T(2,128)} %bitcast.4, f32[121,2,121]{2,1,0:T(2,128)} %bitcast.5, f32[121,2,121]{2,1,0:T(2,128)} %bitcast.6, bf16[27,121,121]{2,1,0:T(8,128)(2,1)} %leaf_any.1, bf16[128,121]{1,0:T(8,128)(2,1)} %ts_any.1, ...), custom_call_target="tpu_custom_call" | custom-call | tf_op jit(solution)/shard_map/pallas_call | solution.py:426
  23.5 0.7 %copy.13 = f32[128,256]{1,0:T(8,128)} copy(f32[128,256]{1,0:T(8,128)S(1)} %shard_map.109) | data formatting | bytes 262144

commit v2 on v1

v2 whole, which is shorter than its diff:
```python
import functools

import jax
import jax.numpy as jnp
from jax import lax
from jax.experimental import pallas as pl
from jax.experimental.pallas import tpu as pltpu
from jax.sharding import PartitionSpec as P

HALO = 32
PEERS = 4
CAP_FAR = 32
LANES = 128
BF = jnp.bfloat16
F32 = jnp.float32
MESH = pl.DeviceIdType.MESH
OFFSETS = tuple(range(-PEERS, 0)) + tuple(range(1, PEERS + 1))


def mm(a, b):
    return jnp.dot(a, b, preferred_element_type=F32)


def halves(x):
    high = x.astype(BF)
    return high, (x - high.astype(F32)).astype(BF)


def one_hot(rows, index):
    count = index.shape[1]
    lines = lax.broadcasted_iota(jnp.int32, (rows, count), 0).astype(F32).astype(BF)
    hit = lines == jnp.broadcast_to(index.astype(BF), (rows, count))
    return jnp.where(hit, jnp.ones((), BF), jnp.zeros((), BF))


def kernel(
    n, cells, cap,
    slip_any, tm_any, up_any, down_any, sib_any, leaf_any, ts_any, nb_any, send_any, far_any, near_any,
    out_ref,
    slip_ref, tm_ref, up_ref, down_ref, sib_ref, leaf_ref, ts_ref, nb_ref, send_ref, far_ref, near_ref,
    far_out, near_out, far_buf, near_buf, edges, halo, root_out, roots, send_f, far_idx,
    weight, w_up, w_sib, w_down, w_up2, w_down2, agg, terms, loc, own_loc, rel, near_rel, source, leaf_cat, columns, near_cols, load_sem,
    above, far_send, far_recv, near_send, near_recv, halo_send, halo_recv, root_send, root_recv,
):
    me = lax.axis_index("leaf")
    coef = tm_ref.shape[0]
    types = far_ref.shape[0]
    kinds = near_ref.shape[0]
    rest = cap - CAP_FAR
    team = 256 // CAP_FAR
    teams = n // team
    mine = me // team
    close = cells + near_buf.shape[0]

    pairs = (
        (slip_any, slip_ref), (tm_any, tm_ref), (send_any, send_ref), (up_any, up_ref), (sib_any, sib_ref),
        (far_any, far_ref), (near_any, near_ref), (down_any, down_ref), (leaf_any, leaf_ref), (nb_any, nb_ref),
        (ts_any, ts_ref),
    )
    loads = [pltpu.make_async_copy(a, b, load_sem.at[i]) for i, (a, b) in enumerate(pairs)]
    for copy in loads:
        copy.start()

    barrier = pltpu.get_barrier_semaphore()

    far_buf[...] = jnp.zeros_like(far_buf)
    near_buf[...] = jnp.zeros_like(near_buf)
    halo[...] = jnp.zeros_like(halo)

    def greet(q, carry):
        pl.semaphore_signal(barrier, inc=1, device_id=(q,), device_id_type=MESH)
        return carry

    lax.fori_loop(me + 1, n, greet, 0)
    @pl.when(me > 0)
    def _():
        pl.semaphore_wait(barrier, me)


    def answer(q, carry):
        pl.semaphore_signal(above.at[mine], inc=1, device_id=(q,), device_id_type=MESH)
        return carry

    lax.fori_loop(0, me, answer, 0)

    weight[...] = jnp.zeros_like(weight)
    w_sib[...] = jnp.zeros_like(w_sib)
    leaf_cat[...] = jnp.zeros_like(leaf_cat)
    for copy in loads[:3]:
        copy.wait()

    weight[0, :coef, :] = tm_ref[...].astype(F32)
    multipole = mm(weight[0].astype(BF), slip_ref[...]).astype(BF)
    source[:, :cells] = multipole
    edges[0] = slip_ref[:, :LANES].astype(F32).T[:HALO].astype(BF)
    edges[1] = slip_ref[:, cells - LANES :].astype(F32).T[LANES - HALO :].astype(BF)

    def far_copy(target):
        return pltpu.make_async_remote_copy(
            src_ref=far_out.at[pl.ds(pl.multiple_of(target * CAP_FAR, CAP_FAR), CAP_FAR)],
            dst_ref=far_buf.at[pl.ds(pl.multiple_of(me * CAP_FAR, CAP_FAR), CAP_FAR)],
            send_sem=far_send,
            recv_sem=far_recv.at[mine],
            device_id=(target,),
            device_id_type=MESH,
        )

    def far_rows(start, rows, team_index):
        return pltpu.make_async_remote_copy(
            src_ref=far_out.at[pl.ds(start, rows)],
            dst_ref=far_buf.at[pl.ds(start, rows)],
            send_sem=far_send,
            recv_sem=far_recv.at[team_index],
            device_id=(lax.rem(me + 1, n),),
            device_id_type=MESH,
        )

    def near_copy(j):
        target = jnp.clip(me + OFFSETS[j], 0, n - 1)
        back = len(OFFSETS) - 1 - j
        return pltpu.make_async_remote_copy(
            src_ref=near_out.at[pl.ds(j * cap + CAP_FAR, rest)],
            dst_ref=near_buf.at[pl.ds(back * rest, rest)],
            send_sem=near_send,
            recv_sem=near_recv,
            device_id=(target,),
            device_id_type=MESH,
        )

    def near_rows(count):
        return pltpu.make_async_remote_copy(
            src_ref=near_out.at[pl.ds(0, count * rest)],
            dst_ref=near_buf.at[pl.ds(0, count * rest)],
            send_sem=near_send,
            recv_sem=near_recv,
            device_id=(lax.rem(me + 1, n),),
            device_id_type=MESH,
        )

    def halo_copy(side):
        target = jnp.clip(me + (1 if side else -1), 0, n - 1)
        return pltpu.make_async_remote_copy(
            src_ref=edges.at[side],
            dst_ref=halo.at[pl.ds((1 - side) * HALO, HALO)],
            send_sem=halo_send.at[side],
            recv_sem=halo_recv.at[1 - side],
            device_id=(target,),
            device_id_type=MESH,
        )

    def root_copy(target):
        return pltpu.make_async_remote_copy(
            src_ref=root_out,
            dst_ref=roots.at[me],
            send_sem=root_send,
            recv_sem=root_recv,
            device_id=(target,),
            device_id_type=MESH,
        )

    def root_rows():
        return pltpu.make_async_remote_copy(
            src_ref=roots.at[pl.ds(0, n - 1)],
            dst_ref=roots.at[pl.ds(0, n - 1)],
            send_sem=root_send,
            recv_sem=root_recv,
            device_id=(lax.rem(me + 1, n),),
            device_id_type=MESH,
        )

    def inside(offset):
        return jnp.logical_and(me + offset >= 0, me + offset < n)

    send_f[...] = send_ref[...].astype(F32)
    per_row = LANES // CAP_FAR
    strip = 8 * per_row
    lane = lax.broadcasted_iota(jnp.int32, (8, LANES), 1)
    for g in range(n // strip):
        packed = send_f[pl.ds(g * strip, 8, stride=per_row), :]
        for j in range(1, per_row):
            shifted = pltpu.roll(send_f[pl.ds(g * strip + j, 8, stride=per_row), :], j * CAP_FAR, axis=1)
            packed = jnp.where(lane >= j * CAP_FAR, shifted, packed)
        far_idx[g * 8 : (g + 1) * 8, :] = packed

    def pick(first, second):
        hits = jnp.concatenate([one_hot(cells, first), one_hot(cells, second)], axis=1)
        return mm(multipole, hits).T.astype(BF)

    def pick_far(g):
        far_out[g * 256 : (g + 1) * 256, :] = pick(far_idx[2 * g : 2 * g + 1, :], far_idx[2 * g + 1 : 2 * g + 2, :])

    def pick_near(j):
        first, second = (
            send_f[pl.ds(jnp.clip(me + OFFSETS[i], 0, n - 1), 1), :] for i in (j, j + 1)
        )
        near_out[j * cap : (j + 2) * cap, :] = pick(first, second)

    for j in range(0, len(OFFSETS), 2):
        pick_near(j)

    def weave(chain, count, fillers):
        done = 0
        for i, _ in enumerate(chain):
            upto = min(len(fillers), -(-len(fillers) * (i + 1) // count))
            for work in fillers[done:upto]:
                work()
            done = upto
        for work in fillers[done:]:
            work()

    def send_far(low, high, lower):
        def step(i, carry):
            target = (i // team) * team + lax.rem(me + i, team)

            @pl.when(target < me if lower else target > me)
            def _():
                far_copy(target).start()

            return carry

        lax.fori_loop(low, high, step, 0)

    def send_near(wanted):
        for j, offset in enumerate(OFFSETS):
            if (offset < 0) == (wanted is None):
                place_of = me + offset
                ready = place_of >= 0 if wanted is None else jnp.logical_and(place_of < n, place_of // team == wanted)

                @pl.when(ready)
                def _():
                    near_copy(j).start()

    def send_root(low, high):
        def step(q, carry):
            root_copy(q).start()
            return carry

        lax.fori_loop(low, high, step, 0)

    @pl.when(inside(-1))
    def _():
        halo_copy(0).start()

    send_near(None)

    for copy in loads[3:8]:
        copy.wait()

    def parts(ref, index):
        weight[index, :coef, :coef] = ref
        weight[index, :coef, coef:] = jnp.zeros((coef, LANES - coef), F32)
        return halves(weight[index].T)

    def product(highs, lows):
        tall = [jnp.concatenate(x, axis=0) for x in (highs, lows)]
        wide = [jnp.concatenate(x, axis=1) for x in (highs, lows)]
        return halves(mm(tall[0], wide[0]) + mm(tall[0], wide[1]) + mm(tall[1], wide[0]))

    ups = [parts(up_ref[:, s, :], s) for s in (0, 1)]
    for s in (0, 1):
        w_up[s * LANES : (s + 1) * LANES, :LANES] = ups[s][0]
        w_up[s * LANES : (s + 1) * LANES, LANES:] = ups[s][1]
    for i, both in enumerate(product(*zip(*ups))):
        for c in range(4):
            w_up2[c * LANES : (c + 1) * LANES, i * LANES : (i + 1) * LANES] = both[
                (c & 1) * LANES : ((c & 1) + 1) * LANES, (c >> 1) * LANES : ((c >> 1) + 1) * LANES
            ]

    def prepare():
        for s in (0, 1):
            high, low = parts(sib_ref[:, s, :], 4 + s)
            other = 1 - s
            w_sib[0, other * LANES : (other + 1) * LANES, s * LANES : (s + 1) * LANES] = high
            w_sib[1, other * LANES : (other + 1) * LANES, s * LANES : (s + 1) * LANES] = low
        downs = [parts(down_ref[:, s, :], 2 + s) for s in (0, 1)]
        for s in (0, 1):
            w_down[:LANES, s * LANES : (s + 1) * LANES] = downs[s][0]
            w_down[LANES:, s * LANES : (s + 1) * LANES] = downs[s][1]
        for i, both in enumerate(product(*zip(*downs))):
            for s in (0, 1):
                w_down2[i * LANES : (i + 1) * LANES, 2 * s * LANES : 2 * (s + 1) * LANES] = both[
                    s * LANES : (s + 1) * LANES, :
                ]

    def pair(base, rows):
        m = max(rows // 2, 8)
        even = agg[pl.ds(base, m, stride=2), :]
        odd = agg[pl.ds(base + 1, m, stride=2), :]
        return m, halves(jnp.concatenate([even, odd], axis=1))

    def lift(base, rows):
        _, (high, low) = pair(base, rows)
        first = mm(high, w_up[...])
        second = mm(low, w_up[:, :LANES])
        return first[:, :LANES] + first[:, LANES:] + second

    def lift2(base, rows):
        m = max(rows // 4, 8)
        four = [agg[pl.ds(base + c, m, stride=4), :] for c in range(4)]
        high, low = halves(jnp.concatenate(four, axis=1))
        first = mm(high, w_up2[...])
        second = mm(low, w_up2[:, :LANES])
        return first[:, :LANES] + first[:, LANES:] + second

    def across(high, low):
        return mm(high, w_sib[0]) + mm(high, w_sib[1]) + mm(low, w_sib[0])

    def place(base, value):
        agg[base : base + value.shape[0], :] = value
        if value.shape[0] < 32:
            agg[base + value.shape[0] : base + 32, :] = jnp.zeros((32 - value.shape[0], LANES), F32)

    local_levels = cells.bit_length() - 1
    tree_bits = n.bit_length() - 1
    agg[:cells, :] = multipole.astype(F32).T
    bases = [0]
    for height in range(local_levels):
        bases.append(bases[-1] + max(cells >> height, 32))
    local_spots = [(base - cells) // 2 for base in bases]

    def spread(start, stop, spot):
        m = (stop - start) // 2
        even = agg[pl.ds(start, m, stride=2), :]
        odd = agg[pl.ds(start + 1, m, stride=2), :]
        terms[spot : spot + m, :] = across(*halves(jnp.concatenate([even, odd], axis=1)))

    def rise(bases, sizes, last):
        for height in range(0, last, 2):
            value = None
            if height + 2 <= last:
                value = lift2(bases[height], sizes[height])
                place(bases[height + 2], value)
            if height + 1 <= last:
                below = lift(bases[height], sizes[height])
                place(bases[height + 1], below)
                value = below if value is None else value
            yield value

    def climb():
        for value in rise(bases, [cells >> h for h in range(local_levels + 1)], local_levels):
            yield
        root_out[...] = value[:1]
        roots[me] = value[:1]

    def beside_own(k):
        near_cols[k * LANES : (k + 1) * LANES, :] = mm(
            slips, one_hot(cells, near_rel[0, k : k + 1, :])
        ).astype(BF)

    def column(t, starts, count, more):
        found = sum(
            mm(
                source[:, pl.ds(pl.multiple_of(low * 256, 256), count * 256)],
                jnp.concatenate([one_hot(256, rel[low + b, t : t + 1, :]) for b in range(count)], axis=0),
            )
            for low in starts
        ).astype(BF)
        if more:
            found = found + columns[t * LANES : (t + 1) * LANES, :]
        columns[t * LANES : (t + 1) * LANES, :] = found

    def columns_of(starts, count, more):
        return [functools.partial(column, t, starts, count, more) for t in range(types)]

    def gather(starts, count, more):
        for work in columns_of(starts, count, more):
            work()

    weave(
        climb(),
        (local_levels + 1) // 2,
        [functools.partial(pick_far, g) for g in range(n // (2 * per_row))],
    )

    send_root(0, me)
    send_far(0, (mine + 1) * team, True)

    @pl.when(lax.rem(me, team) < team - 1)
    def _():
        pl.semaphore_wait(above.at[mine], team - 1 - lax.rem(me, team))

    send_root(me + 1, (mine + 1) * team)
    send_near(mine)
    send_far(mine * team, (mine + 1) * team, False)

    @pl.when(mine + 1 < teams)
    def _():
        pl.semaphore_wait(above.at[mine + 1], team)
        send_root((mine + 1) * team, (mine + 2) * team)
        send_near(mine + 1)
        send_far((mine + 1) * team, (mine + 2) * team, False)

    @pl.when(inside(1))
    def _():
        halo_copy(1).start()

    for copy in loads[8:]:
        copy.wait()

    v = far_ref[...]
    behind = v - cells
    sender = behind // cap
    slot = behind % cap
    delta = sender - me
    hop = jnp.where(delta < 0, delta + PEERS, delta + PEERS - 1)
    position = jnp.where(
        v < cells,
        v,
        jnp.where(
            slot < CAP_FAR,
            close + sender * CAP_FAR + slot,
            cells + hop * rest + slot - CAP_FAR,
        ),
    )
    total = source.shape[1]
    blocks = total // 256
    for b in range(blocks):
        rel[b, :types, :] = jnp.clip(position - 256 * b, -1, 256).astype(F32)

    w = near_ref[...]
    near_rel[0, :kinds, :] = jnp.clip(w - HALO, -1, cells).astype(F32)
    near_rel[1, :kinds, :] = jnp.where(
        w < HALO, w, jnp.where(w >= HALO + cells, w - cells, -1)
    ).astype(F32)
    slips = slip_ref[...]

    def wait_team(index, own):
        start = pl.multiple_of(index * 256, 256)
        if own:
            far_rows(start, 256 - CAP_FAR, index).wait_recv()
        else:
            far_rows(start, 256, index).wait_recv()
        source[:, pl.ds(close + start, 256)] = far_buf[pl.ds(start, 256), :].astype(F32).T.astype(BF)
        return close // 256 + index

    prepare()

    def descend(x):
        high, low = halves(x)
        return mm(high, w_down[:LANES, :]) + mm(high, w_down[LANES:, :]) + mm(low, w_down[:LANES, :])

    def descend2(x):
        high, low = halves(x)
        return mm(high, w_down2[:LANES, :]) + mm(high, w_down2[LANES:, :]) + mm(low, w_down2[:LANES, :])

    def settle():
        spread(bases[1], bases[-1], 0)
        yield
        expansion = None
        for height in reversed(range(local_levels)):
            m = max((cells >> height) // 2, 8)
            both = None if expansion is None else descend(expansion)
            if height >= 1:
                term = terms[local_spots[height] : local_spots[height] + m, :]
                both = term if both is None else both + term
            own_loc[pl.ds(0, m, stride=2), :] = both[:, :LANES]
            own_loc[pl.ds(1, m, stride=2), :] = both[:, LANES:]
            expansion = own_loc[: max(cells >> height, 8), :]
            yield

    def lay(t):
        leaf_cat[:coef, t * LANES : t * LANES + coef] = leaf_ref[t]

    weave(
        settle(),
        local_levels + 1,
        columns_of([0], cells // 256, False)
        + [functools.partial(beside_own, k) for k in range(kinds)]
        + [functools.partial(lay, t) for t in range(types)],
    )

    def send_rest(index, carry):
        pl.semaphore_wait(above.at[index], team)
        send_root(index * team, (index + 1) * team)
        send_far(index * team, (index + 1) * team, False)
        return carry

    lax.fori_loop(mine + 2, teams, send_rest, 0)

    valid = jnp.minimum(me, PEERS) + jnp.minimum(n - 1 - me, PEERS)
    for count in range(PEERS, 2 * PEERS + 1):
        @pl.when(valid == count)
        def _():
            near_rows(count).wait_recv()

    source[:, cells:close] = near_buf[...].astype(F32).T.astype(BF)
    gather([cells // 256], near_buf.shape[0] // 256, True)

    for side in (0, 1):
        @pl.when(inside(-1 if side else 1))
        def _():
            halo_copy(side).wait_recv()

    side_slips = jnp.concatenate(
        [halo[...], jnp.zeros((LANES - 2 * HALO, LANES), BF)], axis=0
    ).astype(F32).T.astype(BF)
    stress = jnp.zeros(out_ref.shape, F32)
    for k in range(kinds):
        beside = near_cols[k * LANES : (k + 1) * LANES, :] + mm(
            side_slips, one_hot(LANES, near_rel[1, k : k + 1, :])
        ).astype(BF)
        stress = stress + mm(nb_ref[k], beside)
    out_ref[...] = stress

    tops = [0]
    for bit in range(tree_bits):
        tops.append(tops[-1] + max(n >> bit, 32))
    top_spot = local_spots[-1]

    def whole_tree():
        place(0, roots[:, 0, :])
        for _ in rise(tops, [n >> bit for bit in range(tree_bits)], tree_bits - 1):
            yield
        spread(0, tops[-1], top_spot)
        yield

        def chosen(bit):
            both = terms[pl.ds(top_spot + tops[bit] // 2 + (me >> (bit + 1)), 1), :]
            both = jnp.broadcast_to(both, (8, 2 * LANES))
            return jnp.where((me >> bit) & 1 == 0, both[:, :LANES], both[:, LANES:])

        def half(both, bit):
            return jnp.where((me >> bit) & 1 == 0, both[:, :LANES], both[:, LANES:])

        line = lax.broadcasted_iota(jnp.int32, (8, LANES), 0)
        expansion = chosen(tree_bits - 1)
        bit = tree_bits - 2
        if tree_bits % 2 == 0 and bit >= 0:
            expansion = half(descend(expansion), bit) + chosen(bit)
            bit -= 1
            yield
        uppers = range(bit, 0, -2)
        aside = jnp.zeros((8, LANES), F32)
        for i, k in enumerate(uppers):
            aside = jnp.where(line == i, chosen(k), aside)
        aside = descend(aside)
        for i, k in enumerate(uppers):
            quarter = descend2(expansion)
            pair_half = jnp.where((me >> k) & 1 == 0, quarter[:, : 2 * LANES], quarter[:, 2 * LANES :])
            pair_half = pair_half + jnp.broadcast_to(aside[i : i + 1, :], pair_half.shape)
            expansion = half(pair_half, k - 1) + chosen(k - 1)
            yield
        rows = 1
        if local_levels % 2:
            both = descend(expansion)
            for c in range(2):
                loc[pl.ds(c, 8, stride=2), :] = both[:, c * LANES : (c + 1) * LANES]
            rows = 2
            expansion = loc[:8, :]
            yield
        while rows < cells:
            m = max(rows, 8)
            four = descend2(expansion)
            for c in range(4):
                loc[pl.ds(c, m, stride=4), :] = four[:, c * LANES : (c + 1) * LANES]
            rows *= 4
            expansion = loc[: max(rows, 8), :]
            yield

    low = wait_team(mine, True)
    root_rows().wait_recv()
    weave(whole_tree(), tree_bits + local_levels // 2, columns_of([low], 1, True))

    def middle(i, carry):
        gather([wait_team(mine ^ i, False)], 1, True)
        return carry

    lax.fori_loop(1, teams - 1, middle, 0)

    gather([wait_team(mine ^ (teams - 1), False)], 1, True)
    leaf_sum = mm(leaf_cat[...], columns[...])
    local_exp = ((loc[...] + own_loc[...]).T + leaf_sum)[:coef].astype(BF)
    out_ref[...] = out_ref[...] + mm(ts_ref[...], local_exp)

    far_rows(0, (n - 1) * CAP_FAR, 0).wait_send()
    root_rows().wait_send()
    for count in range(PEERS, 2 * PEERS + 1):
        @pl.when(valid == count)
        def _():
            near_rows(count).wait_send()

    for side in (0, 1):
        @pl.when(inside(1 if side else -1))
        def _():
            halo_copy(side).wait_send()


def round_up(value, unit):
    return -(-value // unit) * unit


def body(*args):
    args = list(args)
    n = lax.axis_size("leaf")
    cells = args[0].shape[1]
    cap = args[8].shape[1] // n
    for i in (2, 3, 4):
        args[i] = jnp.transpose(args[i], (1, 0, 2))
    args[8] = jnp.reshape(args[8], (n, cap))
    slip, far_list, near_list = args[0], args[9], args[10]
    rest = cap - CAP_FAR
    peers = len(OFFSETS)
    total = cells + n * CAP_FAR + peers * rest
    dma = pltpu.SemaphoreType.DMA
    return pl.pallas_call(
        functools.partial(kernel, n, cells, cap),
        out_shape=pltpu.VMEM(slip.shape, F32),
        in_specs=[pl.BlockSpec(memory_space=pl.ANY)] * len(args),
        out_specs=pl.BlockSpec(memory_space=pltpu.VMEM),
        scratch_shapes=[pltpu.VMEM(a.shape, a.dtype) for a in args] + [
            pltpu.VMEM((n * CAP_FAR, LANES), BF),
            pltpu.VMEM((peers * cap, LANES), BF),
            pltpu.VMEM((n * CAP_FAR, LANES), BF),
            pltpu.VMEM((peers * rest, LANES), BF),
            pltpu.VMEM((2, HALO, LANES), BF),
            pltpu.VMEM((2 * HALO, LANES), BF),
            pltpu.VMEM((1, LANES), F32),
            pltpu.VMEM((n, 1, LANES), F32),
            pltpu.VMEM((n, cap), F32),
            pltpu.VMEM((n * CAP_FAR // LANES, LANES), F32),
            pltpu.VMEM((6, LANES, LANES), F32),
            pltpu.VMEM((2 * LANES, 2 * LANES), BF),
            pltpu.VMEM((2, 2 * LANES, 2 * LANES), BF),
            pltpu.VMEM((2 * LANES, 2 * LANES), BF),
            pltpu.VMEM((4 * LANES, 2 * LANES), BF),
            pltpu.VMEM((2 * LANES, 4 * LANES), BF),
            pltpu.VMEM((2 * cells + 2 * n + 512, LANES), F32),
            pltpu.VMEM((cells + n + 512, 2 * LANES), F32),
            pltpu.VMEM((cells, LANES), F32),
            pltpu.VMEM((cells, LANES), F32),
            pltpu.VMEM((total // 256, round_up(far_list.shape[0], 8), cells), F32),
            pltpu.VMEM((2, round_up(near_list.shape[0], 8), cells), F32),
            pltpu.VMEM((LANES, total), BF),
            pltpu.VMEM((LANES, far_list.shape[0] * LANES), BF),
            pltpu.VMEM((far_list.shape[0] * LANES, cells), BF),
            pltpu.VMEM((near_list.shape[0] * LANES, cells), BF),
            dma((len(args),)),
            pltpu.SemaphoreType.REGULAR((n * CAP_FAR // 256,)),
            dma,
            dma((n * CAP_FAR // 256,)),
            dma,
            dma,
            dma((2,)),
            dma((2,)),
            dma,
            dma,
        ],
        compiler_params=pltpu.CompilerParams(collective_id=0, has_side_effects=True),
    )(*args)


def solution(mesh):
    return jax.shard_map(
        body,
        mesh=mesh,
        in_specs=(
            P(None, "leaf"),
            P(),
            P(),
            P(),
            P(),
            P(),
            P(),
            P(),
            P("leaf", None),
            P(None, "leaf"),
            P(None, "leaf"),
        ),
        out_specs=P(None, "leaf"),
        check_vma=False,
    )
```

time: 24.3 us -> 19.7 us (0.81)
  the two profiles are of different devices: /device:TPU:0 before, /device:TPU:21 now
where the time goes in v2:
time: 19.7 us; the launch traced here: 19.5 us
  Pallas kernels  18.9 us (96%)
  local copies, waits for them, and re-layouts  0.66 us (3%)
    pallas_call x1, Pallas kernels, body(): pl.pallas_call(functools.partial(kernel, n, cells, cap), out_shape=pltpu....  18.9 us
    unnamed x1, local copies, waits for them, and re-layouts  0.66 us

profile of v2, /device:TPU:21, one launch (start us, length us, event | category | flops | bytes accessed | tf_op | source)
XLA Modules:
  0.0 19.5 jit_solution(17308986865567800921)
XLA Ops:
  0.0 18.9 %shard_map.109 = f32[128,256]{1,0:T(8,128)S(1)} custom-call(bf16[128,256]{1,0:T(8,128)(2,1)} %slip_any.1, bf16[121,128]{1,0:T(8,128)(2,1)} %tm_any.1, f32[121,2,121]{2,1,0:T(2,128)} %bitcast.4, f32[121,2,121]{2,1,0:T(2,128)} %bitcast.5, f32[121,2,121]{2,1,0:T(2,128)} %bitcast.6, bf16[27,121,121]{2,1,0:T(8,128)(2,1)} %leaf_any.1, bf16[128,121]{1,0:T(8,128)(2,1)} %ts_any.1, ...), custom_call_target="tpu_custom_call" | custom-call | tf_op jit(solution)/shard_map/pallas_call | solution.py:605
  18.9 0.7 %copy.13 = f32[128,256]{1,0:T(8,128)} copy(f32[128,256]{1,0:T(8,128)S(1)} %shard_map.109) | data formatting | bytes 262144

commit v3 on v2

--- a/solution.py
+++ b/solution.py
@@ -121,21 +121,25 @@
         return pltpu.make_async_remote_copy(
             src_ref=near_out.at[pl.ds(j * cap + CAP_FAR, rest)],
             dst_ref=near_buf.at[pl.ds(back * rest, rest)],
-            send_sem=near_send,
-            recv_sem=near_recv,
+            send_sem=near_send.at[j // PEERS],
+            recv_sem=near_recv.at[back // PEERS],
             device_id=(target,),
             device_id_type=MESH,
         )
 
-    def near_rows(count):
+    def near_rows(side, count):
         return pltpu.make_async_remote_copy(
             src_ref=near_out.at[pl.ds(0, count * rest)],
-            dst_ref=near_buf.at[pl.ds(0, count * rest)],
-            send_sem=near_send,
-            recv_sem=near_recv,
+            dst_ref=near_buf.at[pl.ds(side * PEERS * rest, count * rest)],
+            send_sem=near_send.at[side],
+            recv_sem=near_recv.at[side],
             device_id=(lax.rem(me + 1, n),),
             device_id_type=MESH,
         )
+
+    def near_count(side, count):
+        reach = n - 1 - me if side else me
+        return reach >= count if count == PEERS else reach == count
 
     def halo_copy(side):
         target = jnp.clip(me + (1 if side else -1), 0, n - 1)
@@ -373,26 +377,28 @@
     )
 
     send_root(0, me)
-    send_far(0, (mine + 1) * team, True)
 
     @pl.when(lax.rem(me, team) < team - 1)
     def _():
         pl.semaphore_wait(above.at[mine], team - 1 - lax.rem(me, team))
+        halo_copy(1).start()
 
     send_root(me + 1, (mine + 1) * team)
     send_near(mine)
-    send_far(mine * team, (mine + 1) * team, False)
 
     @pl.when(mine + 1 < teams)
     def _():
         pl.semaphore_wait(above.at[mine + 1], team)
+
+        @pl.when(lax.rem(me, team) == team - 1)
+        def _():
+            halo_copy(1).start()
+
+        send_near(mine + 1)
         send_root((mine + 1) * team, (mine + 2) * team)
-        send_near(mine + 1)
-        send_far((mine + 1) * team, (mine + 2) * team, False)
-
-    @pl.when(inside(1))
-    def _():
-        halo_copy(1).start()
+
+    send_far(0, (mine + 1) * team, True)
+    send_far(mine * team, (mine + 1) * team, False)
 
     for copy in loads[8:]:
         copy.wait()
@@ -469,28 +475,51 @@
         + [functools.partial(lay, t) for t in range(types)],
     )
 
+
     def send_rest(index, carry):
         pl.semaphore_wait(above.at[index], team)
         send_root(index * team, (index + 1) * team)
-        send_far(index * team, (index + 1) * team, False)
         return carry
 
     lax.fori_loop(mine + 2, teams, send_rest, 0)
-
-    valid = jnp.minimum(me, PEERS) + jnp.minimum(n - 1 - me, PEERS)
-    for count in range(PEERS, 2 * PEERS + 1):
-        @pl.when(valid == count)
-        def _():
-            near_rows(count).wait_recv()
-
-    source[:, cells:close] = near_buf[...].astype(F32).T.astype(BF)
-    gather([cells // 256], near_buf.shape[0] // 256, True)
-
+    send_far((mine + 1) * team, n, False)
+
+    def wait_near(side):
+        for count in range(1, PEERS + 1):
+            @pl.when(near_count(side, count))
+            def _():
+                near_rows(side, count).wait_recv()
+
+    def land_near(side):
+        start, rows = side * PEERS * rest, PEERS * rest
+        source[:, cells + start : cells + start + rows] = near_buf[start : start + rows, :].astype(F32).T.astype(BF)
+
+    def near_column(side, t):
+        start = cells + side * PEERS * rest
+        stop = start + PEERS * rest
+        hits = []
+        at = start
+        while at < stop:
+            block, skip = divmod(at, 256)
+            size = min(256 - skip, stop - at)
+            index = rel[block, t : t + 1, :]
+            hits.append(one_hot(size, index - skip if skip else index))
+            at += size
+        found = mm(source[:, start:stop], jnp.concatenate(hits, axis=0)).astype(BF)
+        columns[t * LANES : (t + 1) * LANES, :] = found + columns[t * LANES : (t + 1) * LANES, :]
+
+    wait_near(1)
+    land_near(1)
+    for t in range(types):
+        near_column(1, t)
+
+    wait_near(0)
     for side in (0, 1):
         @pl.when(inside(-1 if side else 1))
         def _():
             halo_copy(side).wait_recv()
 
+    land_near(0)
     side_slips = jnp.concatenate(
         [halo[...], jnp.zeros((LANES - 2 * HALO, LANES), BF)], axis=0
     ).astype(F32).T.astype(BF)
@@ -501,6 +530,8 @@
         ).astype(BF)
         stress = stress + mm(nb_ref[k], beside)
     out_ref[...] = stress
+    for t in range(types):
+        near_column(0, t)
 
     tops = [0]
     for bit in range(tree_bits):
@@ -557,27 +588,46 @@
             expansion = loc[: max(rows, 8), :]
             yield
 
-    low = wait_team(mine, True)
     root_rows().wait_recv()
-    weave(whole_tree(), tree_bits + local_levels // 2, columns_of([low], 1, True))
-
-    def middle(i, carry):
-        gather([wait_team(mine ^ i, False)], 1, True)
-        return carry
-
-    lax.fori_loop(1, teams - 1, middle, 0)
-
-    gather([wait_team(mine ^ (teams - 1), False)], 1, True)
+    weave(
+        whole_tree(),
+        tree_bits + local_levels // 2,
+        columns_of([wait_team(mine, True), wait_team(mine ^ 1, False)], 1, True),
+    )
+
+    def finish(low, following):
+        works = columns_of([low], 1, True)
+        cut = types // 2
+        for work in works[:cut]:
+            work()
+        low = None if following is None else wait_team(following, False)
+        for work in works[cut:]:
+            work()
+        return low
+
+    if teams <= 4:
+        low = wait_team(mine ^ 2, False)
+        for i in range(3, teams):
+            low = finish(low, mine ^ i)
+        finish(low, None)
+    else:
+        def middle(i, carry):
+            gather([wait_team(mine ^ i, False)], 1, True)
+            return carry
+
+        lax.fori_loop(2, teams, middle, 0)
+
     leaf_sum = mm(leaf_cat[...], columns[...])
     local_exp = ((loc[...] + own_loc[...]).T + leaf_sum)[:coef].astype(BF)
     out_ref[...] = out_ref[...] + mm(ts_ref[...], local_exp)
 
     far_rows(0, (n - 1) * CAP_FAR, 0).wait_send()
     root_rows().wait_send()
-    for count in range(PEERS, 2 * PEERS + 1):
-        @pl.when(valid == count)
-        def _():
-            near_rows(count).wait_send()
+    for side in (0, 1):
+        for count in range(1, PEERS + 1):
+            @pl.when(near_count(side, count))
+            def _():
+                near_rows(side, count).wait_send()
 
     for side in (0, 1):
         @pl.when(inside(1 if side else -1))
@@ -638,8 +688,8 @@
             pltpu.SemaphoreType.REGULAR((n * CAP_FAR // 256,)),
             dma,
             dma((n * CAP_FAR // 256,)),
-            dma,
-            dma,
+            dma((2,)),
+            dma((2,)),
             dma((2,)),
             dma((2,)),
             dma,

time: 19.7 us -> 18.3 us (0.929)
  the two profiles are of different devices: /device:TPU:21 before, /device:TPU:25 now
where the time goes in v3:
time: 18.3 us; the launch traced here: 18.2 us
  Pallas kernels  17.5 us (96%)
  local copies, waits for them, and re-layouts  0.66 us (4%)
    pallas_call x1, Pallas kernels, body(): pl.pallas_call(functools.partial(kernel, n, cells, cap), out_shape=pltpu....  17.5 us
    unnamed x1, local copies, waits for them, and re-layouts  0.66 us

profile of v3, /device:TPU:25, one launch (start us, length us, event | category | flops | bytes accessed | tf_op | source)
XLA Modules:
  0.0 18.2 jit_solution(6459224824960711470)
XLA Ops:
  0.0 17.5 %shard_map.109 = f32[128,256]{1,0:T(8,128)S(1)} custom-call(bf16[128,256]{1,0:T(8,128)(2,1)} %slip_any.1, bf16[121,128]{1,0:T(8,128)(2,1)} %tm_any.1, f32[121,2,121]{2,1,0:T(2,128)} %bitcast.4, f32[121,2,121]{2,1,0:T(2,128)} %bitcast.5, f32[121,2,121]{2,1,0:T(2,128)} %bitcast.6, bf16[27,121,121]{2,1,0:T(8,128)(2,1)} %leaf_any.1, bf16[128,121]{1,0:T(8,128)(2,1)} %ts_any.1, ...), custom_call_target="tpu_custom_call" | custom-call | tf_op jit(solution)/shard_map/pallas_call | solution.py:655
  17.5 0.7 %copy.13 = f32[128,256]{1,0:T(8,128)} copy(f32[128,256]{1,0:T(8,128)S(1)} %shard_map.109) | data formatting | bytes 262144

commit v4 on v3

--- a/solution.py
+++ b/solution.py
@@ -72,16 +72,9 @@
         return carry
 
     lax.fori_loop(me + 1, n, greet, 0)
-    @pl.when(me > 0)
-    def _():
-        pl.semaphore_wait(barrier, me)
-
-
     def answer(q, carry):
         pl.semaphore_signal(above.at[mine], inc=1, device_id=(q,), device_id_type=MESH)
         return carry
-
-    lax.fori_loop(0, me, answer, 0)
 
     weight[...] = jnp.zeros_like(weight)
     w_sib[...] = jnp.zeros_like(w_sib)
@@ -214,7 +207,8 @@
 
     def send_far(low, high, lower):
         def step(i, carry):
-            target = (i // team) * team + lax.rem(me + i, team)
+            group = i // team if lower else jnp.where(mine == 0, lax.rem(i // team, teams), mine + teams - i // team)
+            target = group * team + lax.rem(me + i, team)
 
             @pl.when(target < me if lower else target > me)
             def _():
@@ -241,11 +235,20 @@
 
         lax.fori_loop(low, high, step, 0)
 
-    @pl.when(inside(-1))
+    def first_sends():
+        @pl.when(me > 0)
+        def _():
+            pl.semaphore_wait(barrier, me)
+            halo_copy(0).start()
+
+        lax.fori_loop(0, me, answer, 0)
+        send_near(None)
+
+    late = lax.rem(me, team) < 2
+
+    @pl.when(jnp.logical_not(late))
     def _():
-        halo_copy(0).start()
-
-    send_near(None)
+        first_sends()
 
     for copy in loads[3:8]:
         copy.wait()
@@ -376,7 +379,15 @@
         [functools.partial(pick_far, g) for g in range(n // (2 * per_row))],
     )
 
+    @pl.when(late)
+    def _():
+        first_sends()
+
     send_root(0, me)
+
+    @pl.when(mine > 0)
+    def _():
+        send_far(0, team, True)
 
     @pl.when(lax.rem(me, team) < team - 1)
     def _():
@@ -397,8 +408,8 @@
         send_near(mine + 1)
         send_root((mine + 1) * team, (mine + 2) * team)
 
-    send_far(0, (mine + 1) * team, True)
-    send_far(mine * team, (mine + 1) * team, False)
+    send_far(jnp.minimum(mine, 1) * team, (mine + 1) * team, True)
+    send_far(n, n + team, False)
 
     for copy in loads[8:]:
         copy.wait()
@@ -467,14 +478,18 @@
     def lay(t):
         leaf_cat[:coef, t * LANES : t * LANES + coef] = leaf_ref[t]
 
-    weave(
-        settle(),
-        local_levels + 1,
-        columns_of([0], cells // 256, False)
-        + [functools.partial(beside_own, k) for k in range(kinds)]
-        + [functools.partial(lay, t) for t in range(types)],
-    )
-
+    def own_work():
+        weave(
+            settle(),
+            local_levels + 1,
+            columns_of([0], cells // 256, False)
+            + [functools.partial(beside_own, k) for k in range(kinds)]
+            + [functools.partial(lay, t) for t in range(types)],
+        )
+
+    @pl.when(mine == 0)
+    def _():
+        own_work()
 
     def send_rest(index, carry):
         pl.semaphore_wait(above.at[index], team)
@@ -483,6 +498,11 @@
 
     lax.fori_loop(mine + 2, teams, send_rest, 0)
     send_far((mine + 1) * team, n, False)
+
+    @pl.when(mine > 0)
+    def _():
+        own_work()
+
 
     def wait_near(side):
         for count in range(1, PEERS + 1):
@@ -490,28 +510,15 @@
             def _():
                 near_rows(side, count).wait_recv()
 
-    def land_near(side):
-        start, rows = side * PEERS * rest, PEERS * rest
-        source[:, cells + start : cells + start + rows] = near_buf[start : start + rows, :].astype(F32).T.astype(BF)
-
-    def near_column(side, t):
-        start = cells + side * PEERS * rest
-        stop = start + PEERS * rest
-        hits = []
-        at = start
-        while at < stop:
-            block, skip = divmod(at, 256)
-            size = min(256 - skip, stop - at)
-            index = rel[block, t : t + 1, :]
-            hits.append(one_hot(size, index - skip if skip else index))
-            at += size
-        found = mm(source[:, start:stop], jnp.concatenate(hits, axis=0)).astype(BF)
-        columns[t * LANES : (t + 1) * LANES, :] = found + columns[t * LANES : (t + 1) * LANES, :]
+    split = (close - cells) // 2 + cells
+    split = -(-split // 256) * 256
+
+    def land_near(start, stop):
+        source[:, start:stop] = near_buf[start - cells : stop - cells, :].astype(F32).T.astype(BF)
 
     wait_near(1)
-    land_near(1)
-    for t in range(types):
-        near_column(1, t)
+    land_near(split, close)
+    gather([split // 256], (close - split) // 256, True)
 
     wait_near(0)
     for side in (0, 1):
@@ -519,7 +526,7 @@
         def _():
             halo_copy(side).wait_recv()
 
-    land_near(0)
+    land_near(cells, split)
     side_slips = jnp.concatenate(
         [halo[...], jnp.zeros((LANES - 2 * HALO, LANES), BF)], axis=0
     ).astype(F32).T.astype(BF)
@@ -530,8 +537,7 @@
         ).astype(BF)
         stress = stress + mm(nb_ref[k], beside)
     out_ref[...] = stress
-    for t in range(types):
-        near_column(0, t)
+    gather([cells // 256], (split - cells) // 256, True)
 
     tops = [0]
     for bit in range(tree_bits):
@@ -592,7 +598,7 @@
     weave(
         whole_tree(),
         tree_bits + local_levels // 2,
-        columns_of([wait_team(mine, True), wait_team(mine ^ 1, False)], 1, True),
+        columns_of([wait_team(mine, True)], 1, True),
     )
 
     def finish(low, following):
@@ -606,16 +612,17 @@
         return low
 
     if teams <= 4:
-        low = wait_team(mine ^ 2, False)
-        for i in range(3, teams):
+        low = wait_team(mine ^ 1, False)
+        for i in range(2, teams - 1):
             low = finish(low, mine ^ i)
         finish(low, None)
+        finish(wait_team(mine ^ (teams - 1), False), None)
     else:
         def middle(i, carry):
             gather([wait_team(mine ^ i, False)], 1, True)
             return carry
 
-        lax.fori_loop(2, teams, middle, 0)
+        lax.fori_loop(1, teams, middle, 0)
 
     leaf_sum = mm(leaf_cat[...], columns[...])
     local_exp = ((loc[...] + own_loc[...]).T + leaf_sum)[:coef].astype(BF)

time: 18.3 us -> 17.6 us (0.962)
  the two profiles are of different devices: /device:TPU:25 before, /device:TPU:26 now
where the time goes in v4:
time: 17.6 us; the launch traced here: 17.5 us
  Pallas kernels  16.8 us (95%)
  local copies, waits for them, and re-layouts  0.66 us (4%)
    pallas_call x1, Pallas kernels, body(): pl.pallas_call(functools.partial(kernel, n, cells, cap), out_shape=pltpu....  16.8 us
    unnamed x1, local copies, waits for them, and re-layouts  0.66 us

profile of v4, /device:TPU:26, one launch (start us, length us, event | category | flops | bytes accessed | tf_op | source)
XLA Modules:
  0.0 17.5 jit_solution(11739166071695361190)
XLA Ops:
  0.0 16.8 %shard_map.109 = f32[128,256]{1,0:T(8,128)S(1)} custom-call(bf16[128,256]{1,0:T(8,128)(2,1)} %slip_any.1, bf16[121,128]{1,0:T(8,128)(2,1)} %tm_any.1, f32[121,2,121]{2,1,0:T(2,128)} %bitcast.4, f32[121,2,121]{2,1,0:T(2,128)} %bitcast.5, f32[121,2,121]{2,1,0:T(2,128)} %bitcast.6, bf16[27,121,121]{2,1,0:T(8,128)(2,1)} %leaf_any.1, bf16[128,121]{1,0:T(8,128)(2,1)} %ts_any.1, ...), custom_call_target="tpu_custom_call" | custom-call | tf_op jit(solution)/shard_map/pallas_call | solution.py:662
  16.8 0.7 %copy.13 = f32[128,256]{1,0:T(8,128)} copy(f32[128,256]{1,0:T(8,128)S(1)} %shard_map.109) | data formatting | bytes 262144

commit v5 on v4

--- a/solution.py
+++ b/solution.py
@@ -39,7 +39,7 @@
     out_ref,
     slip_ref, tm_ref, up_ref, down_ref, sib_ref, leaf_ref, ts_ref, nb_ref, send_ref, far_ref, near_ref,
     far_out, near_out, far_buf, near_buf, edges, halo, root_out, roots, send_f, far_idx,
-    weight, w_up, w_sib, w_down, w_up2, w_down2, agg, terms, loc, own_loc, rel, near_rel, source, leaf_cat, columns, near_cols, load_sem,
+    weight, w_up, w_sib, w_down, w_up2, w_down2, agg, terms, loc, own_loc, expansion_sum, rel, near_rel, source, leaf_cat, columns, near_cols, load_sem,
     above, far_send, far_recv, near_send, near_recv, halo_send, halo_recv, root_send, root_recv,
 ):
     me = lax.axis_index("leaf")
@@ -601,31 +601,29 @@
         columns_of([wait_team(mine, True)], 1, True),
     )
 
-    def finish(low, following):
-        works = columns_of([low], 1, True)
-        cut = types // 2
-        for work in works[:cut]:
-            work()
-        low = None if following is None else wait_team(following, False)
-        for work in works[cut:]:
-            work()
-        return low
-
     if teams <= 4:
-        low = wait_team(mine ^ 1, False)
-        for i in range(2, teams - 1):
-            low = finish(low, mine ^ i)
-        finish(low, None)
-        finish(wait_team(mine ^ (teams - 1), False), None)
+        gather([wait_team(mine ^ i, False) for i in range(1, teams - 1)], 1, True)
+        last = wait_team(mine ^ (teams - 1), False)
     else:
         def middle(i, carry):
             gather([wait_team(mine ^ i, False)], 1, True)
             return carry
 
-        lax.fori_loop(1, teams, middle, 0)
-
-    leaf_sum = mm(leaf_cat[...], columns[...])
-    local_exp = ((loc[...] + own_loc[...]).T + leaf_sum)[:coef].astype(BF)
+        lax.fori_loop(1, teams - 1, middle, 0)
+        last = wait_team(mine ^ (teams - 1), False)
+
+    expansion_sum[...] = (loc[...] + own_loc[...]).T
+    works = columns_of([last], 1, True)
+    parts_of = 2
+    marks = [types * i // parts_of for i in range(parts_of + 1)]
+    for first, stop in zip(marks[:-1], marks[1:]):
+        for work in works[first:stop]:
+            work()
+        span = slice(first * LANES, stop * LANES)
+        found = expansion_sum[...] + mm(leaf_cat[:, span], columns[span, :])
+        if stop < types:
+            expansion_sum[...] = found
+    local_exp = found[:coef].astype(BF)
     out_ref[...] = out_ref[...] + mm(ts_ref[...], local_exp)
 
     far_rows(0, (n - 1) * CAP_FAR, 0).wait_send()
@@ -685,6 +683,7 @@
             pltpu.VMEM((cells + n + 512, 2 * LANES), F32),
             pltpu.VMEM((cells, LANES), F32),
             pltpu.VMEM((cells, LANES), F32),
+            pltpu.VMEM((LANES, cells), F32),
             pltpu.VMEM((total // 256, round_up(far_list.shape[0], 8), cells), F32),
             pltpu.VMEM((2, round_up(near_list.shape[0], 8), cells), F32),
             pltpu.VMEM((LANES, total), BF),

time: 17.6 us -> 17.4 us (0.989)
  Pallas kernels: 16.8 us -> 16.6 us
    pallas_call x1, Pallas kernels: 16.8 us -> 16.6 us  [body(): pl.pallas_call(functools.partial(kernel, n, cells, cap), out_shape=pltpu....]
where the time goes in v5:
time: 17.4 us; the launch traced here: 17.3 us
  Pallas kernels  16.6 us (95%)
  local copies, waits for them, and re-layouts  0.66 us (4%)
    pallas_call x1, Pallas kernels, body(): pl.pallas_call(functools.partial(kernel, n, cells, cap), out_shape=pltpu....  16.6 us
    unnamed x1, local copies, waits for them, and re-layouts  0.66 us

profile of v5, /device:TPU:26, one launch (start us, length us, event | category | flops | bytes accessed | tf_op | source)
XLA Modules:
  0.0 17.3 jit_solution(14001290026949553271)
XLA Ops:
  0.0 16.6 %shard_map.109 = f32[128,256]{1,0:T(8,128)S(1)} custom-call(bf16[128,256]{1,0:T(8,128)(2,1)} %slip_any.1, bf16[121,128]{1,0:T(8,128)(2,1)} %tm_any.1, f32[121,2,121]{2,1,0:T(2,128)} %bitcast.4, f32[121,2,121]{2,1,0:T(2,128)} %bitcast.5, f32[121,2,121]{2,1,0:T(2,128)} %bitcast.6, bf16[27,121,121]{2,1,0:T(8,128)(2,1)} %leaf_any.1, bf16[128,121]{1,0:T(8,128)(2,1)} %ts_any.1, ...), custom_call_target="tpu_custom_call" | custom-call | tf_op jit(solution)/shard_map/pallas_call | solution.py:660
  16.6 0.7 %copy.13 = f32[128,256]{1,0:T(8,128)} copy(f32[128,256]{1,0:T(8,128)S(1)} %shard_map.109) | data formatting | bytes 262144

commit v6 on v5

--- a/solution.py
+++ b/solution.py
@@ -408,8 +408,16 @@
         send_near(mine + 1)
         send_root((mine + 1) * team, (mine + 2) * team)
 
-    send_far(jnp.minimum(mine, 1) * team, (mine + 1) * team, True)
-    send_far(n, n + team, False)
+    def send_own():
+        send_far(mine * team, (mine + 1) * team, True)
+        send_far(n, n + team, False)
+
+    send_far(jnp.minimum(mine, 1) * team, mine * team, True)
+
+    @pl.when(mine == 0)
+    def _():
+        send_own()
+
 
     for copy in loads[8:]:
         copy.wait()
@@ -498,6 +506,11 @@
 
     lax.fori_loop(mine + 2, teams, send_rest, 0)
     send_far((mine + 1) * team, n, False)
+
+    @pl.when(mine > 0)
+    def _():
+        send_own()
+
 
     @pl.when(mine > 0)
     def _():

time: 17.4 us -> 17.4 us (level)
  no operation moved by 1% of the time
where the time goes in v6:
time: 17.4 us; the launch traced here: 17.2 us
  Pallas kernels  16.6 us (95%)
  local copies, waits for them, and re-layouts  0.66 us (4%)
    pallas_call x1, Pallas kernels, body(): pl.pallas_call(functools.partial(kernel, n, cells, cap), out_shape=pltpu....  16.6 us
    unnamed x1, local copies, waits for them, and re-layouts  0.66 us

profile of v6, /device:TPU:26, one launch (start us, length us, event | category | flops | bytes accessed | tf_op | source)
XLA Modules:
  0.0 17.2 jit_solution(1239937554817660813)
XLA Ops:
  0.0 16.6 %shard_map.109 = f32[128,256]{1,0:T(8,128)S(1)} custom-call(bf16[128,256]{1,0:T(8,128)(2,1)} %slip_any.1, bf16[121,128]{1,0:T(8,128)(2,1)} %tm_any.1, f32[121,2,121]{2,1,0:T(2,128)} %bitcast.4, f32[121,2,121]{2,1,0:T(2,128)} %bitcast.5, f32[121,2,121]{2,1,0:T(2,128)} %bitcast.6, bf16[27,121,121]{2,1,0:T(8,128)(2,1)} %leaf_any.1, bf16[128,121]{1,0:T(8,128)(2,1)} %ts_any.1, ...), custom_call_target="tpu_custom_call" | custom-call | tf_op jit(solution)/shard_map/pallas_call | solution.py:673
  16.6 0.7 %copy.13 = f32[128,256]{1,0:T(8,128)} copy(f32[128,256]{1,0:T(8,128)S(1)} %shard_map.109) | data formatting | bytes 262144
